TPU v7x, 32 devices: a whole 2x2x4 slice. The times are simulated.
32 devices in a mesh: zg: 2 (over x), xy: 16 (over z, y, core).
Axes of the slice: x: 2, y: 2, z: 4, core: 2. Of those that a mesh axis runs over, the one named last changes fastest.
Arguments:
- charges: float32 [65536], P(('zg', 'xy')), may hold values from -12 to 12
- cells: int32 [8, 65536], P(None, ('zg', 'xy')), may hold values from 0 to 3145727
- splines: float32 [8, 65536], P(None, ('zg', 'xy')), may hold values from 0.05 to 1
- counts: int32 [32], P(('zg', 'xy')), may hold values from 1024 to 2048, as said below
- green: bfloat16 [512, 4, 384, 384], P(('zg', 'xy')), may hold values from -0.3125 to 0.3125
Outputs:
- potential: float32 [384, 512, 512], P(('zg', 'xy'))
Inputs may be any that keep to these rules, and one draw needn't show every extreme that they name: `counts`: some device has all 2048 slots live in every draw.
All inputs are finite; a program needn't handle non-finite values.
Results may differ from a plain program's by a relative error of at most 0.0041.
Values may be sent and summed in bfloat16 or wider, within the bound.
A program may use at most 128 MiB of HBM per device.

v0:
```python
import math

import jax
import jax.numpy as jnp
from jax import lax
from jax.sharding import PartitionSpec as P

NX = 512
NY = 512
NZ = 384
KYB = 4
CHUNKS = 2


def tables(length):
    index = jnp.arange(length, dtype=jnp.int32)
    product = index[:, None] * index[None, :] % length
    angle = product.astype(jnp.float32) * (2.0 * math.pi / length)
    return (jnp.cos(angle), jnp.sin(angle))


def product(spec, left, right):
    return jnp.einsum(spec, left, right, preferred_element_type=jnp.float32)


def shards(charges, cells, splines, counts, green):
    devices = lax.axis_size("zg") * lax.axis_size("xy")
    slab = NZ // devices
    waves = NX // devices
    slots = charges.shape[0]
    live = (jnp.arange(slots, dtype=jnp.int32) < counts[0]).astype(jnp.float32)
    values = splines * (charges * live)[None, :]
    density = (
        jnp.zeros((slab * NX * NY,), jnp.float32).at[cells.reshape(-1)].add(values.reshape(-1))
    )
    density = density.reshape(slab, NX, NY)
    cos_y, sin_y = tables(NY)
    cos_x, sin_x = tables(NX)
    scale = 1.0 / math.sqrt(NX * NY)
    forward_y = jnp.stack([cos_y, -sin_y], axis=1)
    forward_x = jnp.stack(
        [jnp.stack([cos_x, sin_x], axis=1), jnp.stack([-sin_x, cos_x], axis=1)], axis=0
    ) * scale
    inverse_x = jnp.stack(
        [jnp.stack([cos_x, -sin_x], axis=1), jnp.stack([sin_x, cos_x], axis=1)], axis=1
    ).astype(jnp.bfloat16)
    inverse_y = jnp.stack([cos_y, -sin_y], axis=0) * scale
    high = lax.Precision.HIGH
    width = NY // CHUNKS
    group = KYB // CHUNKS
    pencils = []
    for part in range(CHUNKS):
        cut = slice(part * width, (part + 1) * width)
        along = jnp.einsum("zxy,yev->zexv", density, forward_y[:, :, cut], precision=high)
        spectrum = jnp.einsum("cuex,zexv->zcuv", forward_x, along, precision=high)
        spectrum = spectrum.astype(jnp.bfloat16)
        spectrum = spectrum.reshape(slab, 2, devices, waves, width).transpose(2, 0, 1, 3, 4)
        pencils.append(
            lax.all_to_all(spectrum, ("zg", "xy"), split_axis=0, concat_axis=0, tiled=True)
        )
    middles = []
    for part in range(CHUNKS):
        blocks = pencils[part].reshape(NZ, 2, waves, group, width // group)
        mixed = product("abzw,wcabj->zcabj", green[:, part * group:(part + 1) * group], blocks)
        mixed = mixed.astype(jnp.bfloat16).reshape(devices, slab, 2, waves, width)
        back = lax.all_to_all(mixed, ("zg", "xy"), split_axis=0, concat_axis=0, tiled=True)
        back = back.transpose(1, 2, 0, 3, 4).reshape(slab, 2, NX, width)
        middles.append(product("xceu,zeuv->zxcv", inverse_x, back).astype(jnp.bfloat16))
    middle = jnp.concatenate(middles, axis=3).astype(jnp.float32)
    return jnp.einsum("zxcv,cvy->zxy", middle, inverse_y, precision=high)


def solution(mesh):
    in_specs = (
        P(("zg", "xy")),
        P(None, ("zg", "xy")),
        P(None, ("zg", "xy")),
        P(("zg", "xy")),
        P(("zg", "xy"), None, None, None),
    )
    out_specs = P(("zg", "xy"), None, None)
    return jax.shard_map(shards, mesh=mesh, in_specs=in_specs, out_specs=out_specs, check_vma=False)
```

profile of v0, /device:TPU:0, one launch (start us, length us, event | category | flops | bytes accessed | tf_op | source)
XLA Modules:
  0.0 785.9 jit_solution(8581125211515026235)
XLA Ops:
  11.2 91.5 %scatter_custom_fusion = f32[3145728]{0:T(1024)} fusion(s32[16384]{0:T(1024)S(1)} %bitcast.140, f32[16384]{0:T(1024)S(1)} %bitcast.139, f32[]{:T(128)} %constant.28.clone.1), kind=kCustom, calls=%fused_computation.31 | custom fusion | flops 16384 | bytes 12582916 | tf_op jit(solution)/shard_map/scatter-add | solution.py:34
  102.6 13.8 %reshape.228 = f32[12,512,512,1]{2,1,0,3:T(8,128)} reshape(f32[3145728]{0:T(1024)} %scatter_custom_fusion) | data formatting | bytes 25165824 | tf_op jit(solution)/shard_map/reshape | solution.py:36
  116.9 14.7 %fusion.10 = f32[2,256,12,512]{3,1,0,2:T(8,128)S(1)} fusion(f32[12,512,512,1]{2,1,0,3:T(8,128)} %reshape.228, f32[512,1,512]{0,2,1:T(8,128)S(1)} %get-tuple-element.8, f32[512,1,512]{0,2,1:T(8,128)S(1)} %get-tuple-element.7), kind=kOutput, calls=%fused_computation.15 | convolution fusion | flops 9663938560 | bytes 27262976 | tf_op jit(solution)/shard_map/zxy,yev->zexv/dot_general | solution.py:54
  131.7 21.7 %fusion.18 = bf16[12,2,512,256]{2,3,1,0:T(8,128)(2,1)} fusion(f32[2,256,12,512]{3,1,0,2:T(8,128)S(1)} %fusion.10, f32[1,512,2,512]{1,3,2,0:T(8,128)S(1)} %get-tuple-element.6, f32[1,512,2,512]{1,3,2,0:T(8,128)S(1)} %get-tuple-element.5), kind=kOutput, calls=%fused_computation.23 | convolution fusion | flops 19332595712 | bytes 23068672 | tf_op jit(solution)/shard_map/cuex,zexv->zcuv/dot_general | solution.py:55
  153.3 8.7 %copy.17 = bf16[12,2,512,256]{3,2,1,0:T(8,128)(2,1)} copy(bf16[12,2,512,256]{2,3,1,0:T(8,128)(2,1)} %fusion.18) | data formatting | bytes 12582912 | tf_op jit(solution)/shard_map/convert_element_type | solution.py:56
  168.4 7.6 all-to-all-start
  176.1 13.3 %fusion.8 = f32[2,256,12,512]{3,1,0,2:T(8,128)S(1)} fusion(f32[12,512,512,1]{2,1,0,3:T(8,128)} %reshape.228, f32[512,1,512]{0,2,1:T(8,128)S(1)} %get-tuple-element.8, f32[512,1,512]{0,2,1:T(8,128)S(1)} %get-tuple-element.7), kind=kOutput, calls=%fused_computation.13 | convolution fusion | flops 9663938560 | bytes 27262976 | tf_op jit(solution)/shard_map/zxy,yev->zexv/dot_general | solution.py:54
  189.4 21.7 %fusion.20 = bf16[12,2,512,256]{2,3,1,0:T(8,128)(2,1)} fusion(f32[2,256,12,512]{3,1,0,2:T(8,128)S(1)} %fusion.8, f32[1,512,2,512]{1,3,2,0:T(8,128)S(1)} %copy-done.4, f32[1,512,2,512]{1,3,2,0:T(8,128)S(1)} %copy-done.2), kind=kOutput, calls=%fused_computation.25 | convolution fusion | flops 19332595712 | bytes 23068672 | tf_op jit(solution)/shard_map/cuex,zexv->zcuv/dot_general | solution.py:55
  211.1 8.7 %copy.25 = bf16[12,2,512,256]{3,2,1,0:T(8,128)(2,1)} copy(bf16[12,2,512,256]{2,3,1,0:T(8,128)(2,1)} %fusion.20) | data formatting | bytes 12582912 | tf_op jit(solution)/shard_map/convert_element_type | solution.py:56
  226.3 89.3 %all-to-all-done = bf16[32,12,2,16,256]{4,3,2,1,0:T(8,128)(2,1)} async-done(((bf16[32,12,2,16,256]{4,3,2,1,0:T(8,128)(2,1)}), bf16[32,12,2,16,256]{4,3,2,1,0:T(8,128)(2,1)}, u32[]{:S(2)}, u32[]{:S(2)}) %all-to-all-start) | async-done | bytes 6291488 | tf_op jit(solution)/shard_map/all_to_all | solution.py:59
  319.6 9.7 %reshape.212 = bf16[384,2,16,2,128]{4,3,2,1,0:T(2,128)(2,1)} reshape(bf16[32,12,2,16,256]{4,3,2,1,0:T(8,128)(2,1)} %all-to-all-done) | data formatting | bytes 12582912 | tf_op jit(solution)/shard_map/reshape | solution.py:63
  329.3 15.0 %convert_bitcast_fusion.1 = bf16[384,2,16,2,128]{0,4,1,3,2:T(8,128)(2,1)} fusion(bf16[16,4,384,384]{3,2,1,0:T(8,128)(2,1)} %param.9, bf16[384,2,16,2,128]{4,3,2,1,0:T(2,128)(2,1)} %reshape.212), kind=kOutput, calls=%fused_computation.30 | convolution fusion | flops 2419064832 | bytes 22020096 | tf_op jit(solution)/shard_map/abzw,wcabj->zcabj/dot_general | solution.py:23
  344.3 16.3 %copy.20 = bf16[384,2,16,2,128]{4,3,2,1,0:T(2,128)(2,1)} copy(bf16[384,2,16,2,128]{0,4,1,3,2:T(8,128)(2,1)} %convert_bitcast_fusion.1) | data formatting | bytes 12582912 | tf_op jit(solution)/shard_map/convert_element_type | solution.py:65
  360.6 10.9 %reshape.213 = bf16[32,12,2,16,256]{4,3,2,1,0:T(8,128)(2,1)} reshape(bf16[384,2,16,2,128]{4,3,2,1,0:T(2,128)(2,1)} %copy.20) | data formatting | bytes 12582912 | tf_op jit(solution)/shard_map/reshape | solution.py:65
  371.5 87.7 %all-to-all-done.2 = bf16[32,12,2,16,256]{4,3,2,1,0:T(8,128)(2,1)} async-done(((bf16[32,12,2,16,256]{4,3,2,1,0:T(8,128)(2,1)}), bf16[32,12,2,16,256]{4,3,2,1,0:T(8,128)(2,1)}, u32[]{:S(2)}, u32[]{:S(2)}) %all-to-all-start.2) | async-done | bytes 6291488 | tf_op jit(solution)/shard_map/all_to_all | solution.py:59
  462.8 9.7 %reshape.216 = bf16[384,2,16,2,128]{4,3,2,1,0:T(2,128)(2,1)} reshape(bf16[32,12,2,16,256]{4,3,2,1,0:T(8,128)(2,1)} %all-to-all-done.2) | data formatting | bytes 12582912 | tf_op jit(solution)/shard_map/reshape | solution.py:63
  472.5 15.0 %convert_bitcast_fusion = bf16[384,2,16,2,128]{0,4,1,3,2:T(8,128)(2,1)} fusion(bf16[16,4,384,384]{3,2,1,0:T(8,128)(2,1)} %param.9, bf16[384,2,16,2,128]{4,3,2,1,0:T(2,128)(2,1)} %reshape.216), kind=kOutput, calls=%fused_computation.29 | convolution fusion | flops 2419064832 | bytes 22020096 | tf_op jit(solution)/shard_map/abzw,wcabj->zcabj/dot_general | solution.py:23
  487.5 16.1 %copy.28 = bf16[384,2,16,2,128]{4,3,2,1,0:T(2,128)(2,1)} copy(bf16[384,2,16,2,128]{0,4,1,3,2:T(8,128)(2,1)} %convert_bitcast_fusion) | data formatting | bytes 12582912 | tf_op jit(solution)/shard_map/convert_element_type | solution.py:65
  503.6 10.8 %reshape.217 = bf16[32,12,2,16,256]{4,3,2,1,0:T(8,128)(2,1)} reshape(bf16[384,2,16,2,128]{4,3,2,1,0:T(2,128)(2,1)} %copy.28) | data formatting | bytes 12582912 | tf_op jit(solution)/shard_map/reshape | solution.py:65
  514.4 87.9 %all-to-all-done.1 = bf16[32,12,2,16,256]{4,3,2,1,0:T(8,128)(2,1)} async-done(((bf16[32,12,2,16,256]{4,3,2,1,0:T(8,128)(2,1)}), bf16[32,12,2,16,256]{4,3,2,1,0:T(8,128)(2,1)}, u32[]{:S(2)}, u32[]{:S(2)}) %all-to-all-start.1) | async-done | bytes 6291488 | tf_op jit(solution)/shard_map/all_to_all | solution.py:66
  622.3 123.4 %all-to-all-done.3 = bf16[32,12,2,16,256]{4,3,2,1,0:T(8,128)(2,1)} async-done(((bf16[32,12,2,16,256]{4,3,2,1,0:T(8,128)(2,1)}), bf16[32,12,2,16,256]{4,3,2,1,0:T(8,128)(2,1)}, u32[]{:S(2)}, u32[]{:S(2)}) %all-to-all-start.3) | async-done | bytes 6291488 | tf_op jit(solution)/shard_map/all_to_all | solution.py:66
  750.2 8.9 %fusion.19 = bf16[12,512,2,256]{1,3,2,0:T(8,128)(2,1)} fusion(bf16[12,2,512,256,1]{3,2,1,4,0:T(8,128)(2,1)S(1)} %bitcast.135, bf16[512,1,2,512]{0,3,2,1:T(8,128)(2,1)S(1)} %maximum_bitcast_fusion.4, bf16[512,1,2,512]{0,3,2,1:T(8,128)(2,1)S(1)} %fusion.58), kind=kOutput, calls=%fused_computation.24 | convolution fusion | flops 6449790976 | bytes 14680064 | tf_op jit(solution)/shard_map/xceu,zeuv->zxcv/dot_general | solution.py:23
  759.1 8.9 %fusion.21 = bf16[12,512,2,256]{1,3,2,0:T(8,128)(2,1)} fusion(bf16[12,2,512,256,1]{3,2,1,4,0:T(8,128)(2,1)S(1)} %bitcast.136, bf16[512,1,2,512]{0,3,2,1:T(8,128)(2,1)S(1)} %maximum_bitcast_fusion.4, bf16[512,1,2,512]{0,3,2,1:T(8,128)(2,1)S(1)} %fusion.58), kind=kOutput, calls=%fused_computation.26 | convolution fusion | flops 6449790976 | bytes 14680064 | tf_op jit(solution)/shard_map/xceu,zeuv->zxcv/dot_general | solution.py:23
  768.0 17.6 %fusion.30 = f32[12,512,512]{2,1,0:T(8,128)} fusion(bf16[12,512,2,256]{1,3,2,0:T(8,128)(2,1)} %fusion.21, bf16[12,512,2,256]{1,3,2,0:T(8,128)(2,1)S(1)} %copy-done.6, f32[1,512,512]{2,1,0:T(8,128)S(1)} %get-tuple-element.11, f32[1,512,512]{2,1,0:T(8,128)S(1)} %copy-done.5), kind=kOutput, calls=%fused_computation.33 | convolution fusion | flops 19353567232 | bytes 27262976 | tf_op jit(solution)/shard_map/zxcv,cvy->zxy/dot_general | solution.py:70
  (33 shorter events, 56.0 us)
Async XLA Ops:
  116.9 14.7 %copy-start.1 = (f32[1,512,2,512]{1,3,2,0:T(8,128)}, f32[1,512,2,512]{1,3,2,0:T(8,128)S(1)}, u32[]{:S(2)}) copy-start(f32[1,512,2,512]{1,3,2,0:T(8,128)S(1)} %get-tuple-element.5) | copy-start | bytes 6291460
  116.9 14.7 %copy-start.3 = (f32[1,512,2,512]{1,3,2,0:T(8,128)}, f32[1,512,2,512]{1,3,2,0:T(8,128)S(1)}, u32[]{:S(2)}) copy-start(f32[1,512,2,512]{1,3,2,0:T(8,128)S(1)} %get-tuple-element.6) | copy-start | bytes 6291460
  168.4 147.2 %all-to-all-start = ((bf16[32,12,2,16,256]{4,3,2,1,0:T(8,128)(2,1)}), bf16[32,12,2,16,256]{4,3,2,1,0:T(8,128)(2,1)}, u32[]{:S(2)}, u32[]{:S(2)}) async-start(bf16[32,12,2,16,256]{4,3,2,1,0:T(8,128)(2,1)} %copy.18), calls=%async_computation | async-start | bytes 12582912 | tf_op jit(solution)/shard_map/all_to_all | solution.py:59
  176.1 13.4 %copy-start.2 = (f32[1,512,2,512]{1,3,2,0:T(8,128)S(1)}, f32[1,512,2,512]{1,3,2,0:T(8,128)}, u32[]{:S(2)}) copy-start(f32[1,512,2,512]{1,3,2,0:T(8,128)} %copy-done.1) | copy-start | bytes 6291460
  176.1 13.4 %copy-start.4 = (f32[1,512,2,512]{1,3,2,0:T(8,128)S(1)}, f32[1,512,2,512]{1,3,2,0:T(8,128)}, u32[]{:S(2)}) copy-start(f32[1,512,2,512]{1,3,2,0:T(8,128)} %copy-done.3) | copy-start | bytes 6291460
  315.6 143.6 %all-to-all-start.2 = ((bf16[32,12,2,16,256]{4,3,2,1,0:T(8,128)(2,1)}), bf16[32,12,2,16,256]{4,3,2,1,0:T(8,128)(2,1)}, u32[]{:S(2)}, u32[]{:S(2)}) async-start(bf16[32,12,2,16,256]{4,3,2,1,0:T(8,128)(2,1)} %copy.26), calls=%async_computation.2 | async-start | bytes 12582912 | tf_op jit(solution)/shard_map/all_to_all | solution.py:59
  459.1 143.2 %all-to-all-start.1 = ((bf16[32,12,2,16,256]{4,3,2,1,0:T(8,128)(2,1)}), bf16[32,12,2,16,256]{4,3,2,1,0:T(8,128)(2,1)}, u32[]{:S(2)}, u32[]{:S(2)}) async-start(bf16[32,12,2,16,256]{4,3,2,1,0:T(8,128)(2,1)} %reshape.213), calls=%async_computation.1 | async-start | bytes 12582912 | tf_op jit(solution)/shard_map/all_to_all | solution.py:66
  602.3 143.3 %all-to-all-start.3 = ((bf16[32,12,2,16,256]{4,3,2,1,0:T(8,128)(2,1)}), bf16[32,12,2,16,256]{4,3,2,1,0:T(8,128)(2,1)}, u32[]{:S(2)}, u32[]{:S(2)}) async-start(bf16[32,12,2,16,256]{4,3,2,1,0:T(8,128)(2,1)} %reshape.217), calls=%async_computation.3 | async-start | bytes 12582912 | tf_op jit(solution)/shard_map/all_to_all | solution.py:66
  745.6 4.6 copy-start
  759.1 8.9 %copy-start.5 = (f32[1,512,512]{2,1,0:T(8,128)S(1)}, f32[1,512,512]{2,1,0:T(8,128)}, u32[]{:S(2)}) copy-start(f32[1,512,512]{2,1,0:T(8,128)} %get-tuple-element.12) | copy-start | bytes 3145732
  759.1 8.9 %copy-start.6 = (bf16[12,512,2,256]{1,3,2,0:T(8,128)(2,1)S(1)}, bf16[12,512,2,256]{1,3,2,0:T(8,128)(2,1)}, u32[]{:S(2)}) copy-start(bf16[12,512,2,256]{1,3,2,0:T(8,128)(2,1)} %fusion.19) | copy-start | bytes 18874372
where the time goes:
time: 797 us; the launch traced here: 786 us
  waiting for transfers between devices  388 us (49%)
  matrix products  137 us (17%)
  local copies, waits for them, and re-layouts  129 us (16%)
  other arithmetic  111 us (14%)
  starting transfers between devices  19.1 us (2%)
    all_to_all x2, waiting for transfers between devices, shards(): lax.all_to_all(mixed, ('zg', 'xy'), split_axis=0, concat_axis=0, tiled=True)  211 us
    all_to_all x2, waiting for transfers between devices, shards(): lax.all_to_all(spectrum, ('zg', 'xy'), split_axis=0, concat_axis=0, tiled...  177 us
    scatter-add x1, other arithmetic, shards(): jnp.zeros((slab * NX * NY,), jnp.float32).at[cells.reshape(-1)]  91.5 us
    dot_general x4, matrix products, product(): return jnp.einsum(spec, left, right, preferred_element_type=jnp.float32)  47.8 us
    dot_general x2, matrix products, shards(): spectrum = jnp.einsum('cuex,zexv->zcuv', forward_x, along, precision=high)  43.3 us
    convert_element_type x2, local copies, waits for them, and re-layouts, shards(): mixed = mixed.astype(jnp.bfloat16).reshape(devices, slab, 2, waves, width)  32.4 us
    dot_general x2, matrix products, shards(): jnp.einsum('zxy,yev->zexv', density, forward_y[:, :, cut], precision=high)  28 us
    reshape x2, local copies, waits for them, and re-layouts, shards(): mixed = mixed.astype(jnp.bfloat16).reshape(devices, slab, 2, waves, width)  21.7 us
  transfers between devices with their start and end apart: 4, of which 4 were waited for; matrix products, arithmetic and copies ran while one was open for 22% of the time, Pallas kernels for 0%

commit v1 on v0

v1 whole, which is shorter than its diff:
```python
import functools
import math

import jax
import jax.numpy as jnp
import numpy as np
from jax import lax
from jax.experimental import pallas as pl
from jax.experimental.pallas import tpu as pltpu
from jax.sharding import PartitionSpec as P


F32 = jnp.float32
BF16 = jnp.bfloat16
LANES = 128
POINTS = 512
SIDE = 256
VMEM = 60 * 2**20
AXES = ("zg", "xy")


def round_up(value, to):
    return -(-value // to) * to


def split(value):
    high = value.astype(BF16)
    return high, (value - high.astype(F32)).astype(BF16)


def dot(left, right):
    return jnp.dot(left, right, preferred_element_type=F32)


def table(length, block):
    index = np.arange(length)
    angle = (index[:, None] * index[None, :] % length) * (2.0 * math.pi / length)
    blocks = np.stack(
        [np.cos(angle).reshape(length, -1, block), np.sin(angle).reshape(length, -1, block)], axis=2
    ).reshape(length, -1)
    high = blocks.astype(np.float32).astype(BF16)
    low = (blocks - high.astype(np.float64)).astype(np.float32).astype(BF16)
    return high, low


def density_kernel(starts, cells, values, high_ref, low_ref, total):
    who, plane = pl.program_id(0), pl.program_id(1)
    buckets, _, side = total.shape
    rows = high_ref.shape[1] // buckets
    width = side // rows
    names = lax.broadcasted_iota(jnp.int32, (side, POINTS), 0)

    def product(bucket, piece):
        lines = range(POINTS // LANES)
        cell = jnp.concatenate([cells[0, pl.ds(piece + k, 1), :] for k in lines], axis=1)
        value = jnp.concatenate([values[0, pl.ds(piece + k, 1), :] for k in lines], axis=1)
        cell = cell - bucket * (side * side)
        inside = (cell >= 0) & (cell < side * side)
        row = cell // side
        row = (row % width) * rows + row // width
        hit = names == jnp.where(inside, row, -1)
        high = value.astype(BF16).astype(F32)
        low = value - high
        left = jnp.concatenate(
            [jnp.where(hit, high, 0.0).astype(BF16), jnp.where(hit, low, 0.0).astype(BF16)], axis=0
        )
        right = jnp.where(names == (cell & (side - 1)), 1.0, 0.0).astype(BF16)
        return lax.dot_general(left, right, (((1,), (1,)), ((), ())), preferred_element_type=F32)

    for k in range(buckets):
        total[k] = product(plane * buckets + k, starts[who, plane * buckets + k] // LANES)
    for k in range(buckets):
        bucket = plane * buckets + k
        start = starts[who, bucket] // LANES

        def step(turn, carry, k=k, bucket=bucket, start=start):
            total[k] += product(bucket, start + turn * (POINTS // LANES))
            return carry

        lax.fori_loop(1, (starts[who, bucket + 1] - start * LANES + POINTS - 1) // POINTS, step, 0)
    for k in range(buckets):
        block = total[k, :side, :] + total[k, side:, :]
        for part in range(width):
            high, low = split(block[part * rows:(part + 1) * rows, :])
            place = (0, slice(k * rows, (k + 1) * rows), slice(part * side, (part + 1) * side))
            high_ref[place] = high
            low_ref[place] = low


def make_density(starts, cells, values, slab, nx, ny):
    side = SIDE
    buckets = nx * ny // (side * side)
    spec = pl.BlockSpec((1,) + cells.shape[1:], lambda w, z, s: (w, 0, 0))
    out = pl.BlockSpec((1, nx, ny), lambda w, z, s: (w * slab + z, 0, 0))
    shape = jax.ShapeDtypeStruct((2 * slab, nx, ny), BF16)
    return pl.pallas_call(
        density_kernel,
        out_shape=(shape, shape),
        grid_spec=pltpu.PrefetchScalarGridSpec(
            num_scalar_prefetch=1,
            grid=(2, slab),
            in_specs=[spec, spec],
            out_specs=(out, out),
            scratch_shapes=[pltpu.VMEM((buckets, 2 * side, side), F32)],
        ),
        cost_estimate=pl.CostEstimate(
            flops=2 * slab * buckets * 4 * side * side * POINTS, bytes_accessed=8 * slab * nx * ny, transcendentals=0
        ),
        compiler_params=pltpu.CompilerParams(vmem_limit_bytes=VMEM),
        name="density",
    )(starts, cells, values)


def forward_kernel(places, scale, high_ref, low_ref, y_table, x_table, out_ref, real, imag):
    turn = pl.program_id(0)
    planes = high_ref.shape[0]
    stride = out_ref.shape[2]
    half = x_table.shape[0] // 2
    pieces = []
    for k in range(planes):
        left = jnp.concatenate([high_ref[k], low_ref[k], high_ref[k]], axis=1)
        high, low = split(dot(left, y_table[...]))
        pieces.append(jnp.concatenate([high, low, high], axis=0))
    both = dot(x_table[...], jnp.concatenate(pieces, axis=1)) * scale
    for k in range(planes):
        cut = both[:, k * 2 * LANES:(k + 1) * 2 * LANES]
        rows = pl.ds(places[turn * planes + k], half, stride=stride)
        real[rows, :] = cut[:half, :LANES] - cut[half:, LANES:]
        imag[rows, :] = -(cut[:half, LANES:] + cut[half:, :LANES])

    @pl.when(turn == pl.num_programs(0) - 1)
    def _():
        owners, waves = out_ref.shape[0], out_ref.shape[1]
        count = waves * stride

        def step(owner, carry):
            rows = pl.ds(pl.multiple_of(owner * count, 8), count)
            out_ref[owner, :, :, :LANES] = real[rows, :].reshape(waves, stride, LANES).astype(BF16)
            out_ref[owner, :, :, LANES:] = imag[rows, :].reshape(waves, stride, LANES).astype(BF16)
            return carry

        lax.fori_loop(0, owners, step, 0)


def make_forward(places, density, y_table, x_table, block, owners, waves, stride, scale):
    planes, nx, ny = density[0].shape
    half = owners * waves
    plane = pl.BlockSpec((2, nx, ny), lambda p, s: (p, 0, 0))
    shape = (owners, waves, stride, 2 * LANES)
    return pl.pallas_call(
        lambda places, *refs: forward_kernel(places, scale, *refs),
        out_shape=jax.ShapeDtypeStruct(shape, BF16),
        grid_spec=pltpu.PrefetchScalarGridSpec(
            num_scalar_prefetch=1,
            grid=(planes // 2,),
            in_specs=[
                plane,
                plane,
                pl.BlockSpec((3 * ny, 2 * LANES), lambda p, s: (0, block)),
                pl.BlockSpec(x_table.shape, lambda p, s: (0, 0)),
            ],
            out_specs=pl.BlockSpec(shape, lambda p, s: (0, 0, 0, 0)),
            scratch_shapes=[pltpu.VMEM((half * stride, LANES), F32)] * 2,
        ),
        cost_estimate=pl.CostEstimate(
            flops=2 * planes * 3 * 2 * nx * ny * 2 * LANES, bytes_accessed=4 * planes * nx * ny, transcendentals=0
        ),
        compiler_params=pltpu.CompilerParams(vmem_limit_bytes=VMEM),
        name="forward",
    )(places, *density, y_table, x_table)


def mix_kernel(green_ref, seen_ref, order_ref, out_ref, real, imag):
    mix(dot(green_ref[0, 0], arranged(order_ref, seen_ref).astype(BF16)), out_ref, real, imag)


def arranged(order_ref, seen_ref):
    seen = seen_ref[:, 0, :, :].astype(F32)
    seen = seen.reshape(seen.shape[0] * seen.shape[1], seen.shape[2]).astype(BF16)
    return dot(order_ref[...], seen)


def mix(mixed, out_ref, real, imag):
    turn = pl.program_id(0)
    groups, planes, waves, _ = out_ref.shape
    depth = groups * planes
    stride = real.shape[0] // depth
    rows = pl.ds(turn, depth, stride=stride)
    real[rows, :] = mixed[:, :LANES]
    imag[rows, :] = mixed[:, LANES:]

    @pl.when(turn == pl.num_programs(0) - 1)
    def _():
        def step(group, carry):
            for plane in range(planes):
                rows = pl.ds(pl.multiple_of((group * planes + plane) * stride, 8), waves)
                out_ref[group, plane, :, :LANES] = real[rows, :].astype(BF16)
                out_ref[group, plane, :, LANES:] = imag[rows, :].astype(BF16)
            return carry

        lax.fori_loop(0, groups, step, 0)


def mix_block(green, seen, order, block, devices, slab):
    waves, _, depth, _ = green.shape
    groups, _, rows, width = seen.shape
    padded = round_up(waves, 8)
    shape = (devices, slab, padded, width)
    stride = padded if padded % 16 else padded + 8
    return pl.pallas_call(
        mix_kernel,
        out_shape=jax.ShapeDtypeStruct(shape, BF16),
        grid=(waves,),
        in_specs=[
            pl.BlockSpec((1, 1, depth, depth), lambda u: (u, block, 0, 0)),
            pl.BlockSpec((groups, 1, rows, width), lambda u: (0, u, 0, 0)),
            pl.BlockSpec(order.shape, lambda u: (0, 0)),
        ],
        out_specs=pl.BlockSpec(shape, lambda u: (0, 0, 0, 0)),
        scratch_shapes=[pltpu.VMEM((depth * stride, LANES), F32)] * 2,
        cost_estimate=pl.CostEstimate(
            flops=waves * 4 * depth * depth * width,
            bytes_accessed=2 * waves * depth * (depth + 2 * width), transcendentals=0,
        ),
        compiler_params=pltpu.CompilerParams(vmem_limit_bytes=VMEM),
        name="mix",
    )(green, seen, order)


def after(value, other):
    return pl.pallas_call(
        lambda value_ref, other_ref, out_ref: None,
        out_shape=jax.ShapeDtypeStruct(value.shape, value.dtype),
        in_specs=[pl.BlockSpec(memory_space=pl.ANY)] * 2,
        out_specs=pl.BlockSpec(memory_space=pl.ANY),
        input_output_aliases={0: 0},
        name="after",
    )(value, other)


def inverse_kernel(scale, first, *refs):
    if first:
        seen_ref, x_table, y_table, out_ref = refs
    else:
        seen_ref, x_table, y_table, so_far, out_ref = refs
    value = seen_ref[:, 0, :, :]
    both = dot(x_table[...], value.reshape(value.shape[0] * value.shape[1], value.shape[2]))
    nx = both.shape[0] // 2
    real = both[:nx, :LANES] - both[nx:, LANES:]
    imag = -(both[:nx, LANES:] + both[nx:, :LANES])
    middle = (jnp.concatenate([real, imag], axis=1) * scale).astype(BF16)
    result = dot(middle, y_table[0])
    if not first:
        result += so_far[0]
    out_ref[0] = result


def make_inverse(seen, x_table, y_table, block, so_far, scale):
    devices, slab, padded, width = seen.shape
    nx = x_table.shape[0] // 2
    ny = y_table.shape[2]
    out = pl.BlockSpec((1, nx, ny), lambda p: (p, 0, 0))
    first = so_far is None
    return pl.pallas_call(
        functools.partial(inverse_kernel, scale, first),
        out_shape=jax.ShapeDtypeStruct((slab, nx, ny), F32),
        grid=(slab,),
        in_specs=[
            pl.BlockSpec((devices, 1, padded, width), lambda p: (0, p, 0, 0)),
            pl.BlockSpec(x_table.shape, lambda p: (0, 0)),
            pl.BlockSpec((1, 2 * LANES, ny), lambda p: (block, 0, 0)),
        ]
        + ([] if first else [out]),
        out_specs=out,
        input_output_aliases={} if first else {3: 0},
        cost_estimate=pl.CostEstimate(
            flops=2 * slab * nx * width * (2 * nx + ny), bytes_accessed=8 * slab * nx * ny, transcendentals=0
        ),
        compiler_params=pltpu.CompilerParams(vmem_limit_bytes=VMEM),
        name="inverse",
    )(seen, x_table, y_table, *([] if first else [so_far]))


def shards(nx, ny, charges, cells, splines, counts, green):
    n_zg, n_xy = lax.axis_size("zg"), lax.axis_size("xy")
    devices = n_zg * n_xy
    inner = n_xy // 2
    owners = devices // 2
    depth = green.shape[2]
    blocks = green.shape[1]
    slab = depth // devices
    waves = nx // devices
    stride = round_up(2 * slab, 8)
    padded = round_up(waves, 8)
    side = lax.axis_index("xy") // inner
    swap = [(i, (i + inner) % n_xy) for i in range(n_xy)]
    groups = [
        [g * n_xy + s * inner + r for g in range(n_zg) for r in range(inner)] for s in range(2)
    ]
    scale = 1.0 / math.sqrt(nx * ny)

    slots = charges.shape[0]
    live = (jnp.arange(slots, dtype=jnp.int32) < counts[0]).astype(F32)
    values = splines * (charges * live)[None, :]
    sorted_cells, sorted_values = lax.sort((cells.reshape(-1), values.reshape(-1)), num_keys=1, is_stable=False)
    other_cells = lax.ppermute(sorted_cells, "xy", swap)
    other_values = lax.ppermute(sorted_values, "xy", swap)
    both_cells = jnp.where(
        side == 0, jnp.stack([sorted_cells, other_cells]), jnp.stack([other_cells, sorted_cells])
    )
    both_values = jnp.where(
        side == 0, jnp.stack([sorted_values, other_values]), jnp.stack([other_values, sorted_values])
    )
    size = SIDE * SIDE
    edges = jnp.arange(slab * nx * ny // size + 1, dtype=jnp.int32) * size
    starts = jnp.sum((both_cells[:, None, :] < edges[None, :, None]).astype(jnp.int32), axis=2)
    both_cells = jnp.pad(both_cells, ((0, 0), (0, POINTS)), constant_values=-1)
    both_values = jnp.pad(both_values, ((0, 0), (0, POINTS)))
    density = make_density(starts, both_cells.reshape(2, -1, LANES), both_values.reshape(2, -1, LANES), slab, nx, ny)

    high, low = table(ny, LANES)
    y_high, y_low = jnp.asarray(high), jnp.asarray(low)

    def trig(name):
        parts = name.reshape(ny, blocks, 2, LANES)
        return parts[:, :, 0, :].reshape(ny, ny), parts[:, :, 1, :].reshape(ny, ny)

    cos_high, sin_high = trig(y_high)
    cos_low, sin_low = trig(y_low)

    def rows_of(value, half):
        value = value.reshape(n_zg, 2, inner * waves, nx)
        return lax.dynamic_index_in_dim(value, half, 1, keepdims=False).reshape(owners * waves, nx)

    x_high = jnp.concatenate([rows_of(cos_high, side), rows_of(sin_high, side)])
    x_low = jnp.concatenate([rows_of(cos_low, side), rows_of(sin_low, side)])
    x_forward = jnp.concatenate([x_high, x_high, x_low], axis=1)
    y_forward = jnp.concatenate([y_high, y_high, y_low], axis=0)

    def inverse_table(value):
        value = jnp.pad(value.reshape(nx, devices, waves), ((0, 0), (0, 0), (0, padded - waves)))
        return value.reshape(nx, devices * padded)

    x_inverse = jnp.concatenate([inverse_table(cos_high), inverse_table(sin_high)])
    y_inverse = jnp.concatenate(
        [cos_high.reshape(blocks, LANES, ny), sin_high.reshape(blocks, LANES, ny)], axis=1
    )

    place = np.full((n_zg, inner, stride), -1)
    for half in range(2):
        ids = (np.arange(n_zg)[:, None] * 2 + half) * inner + np.arange(inner)[None, :]
        place[:, :, half * slab:(half + 1) * slab] = ids[:, :, None] * slab + np.arange(slab)
    order = (jnp.arange(depth)[:, None] == jnp.asarray(place.reshape(-1))[None, :]).astype(BF16)

    places = jnp.arange(2 * slab, dtype=jnp.int32)

    def exchange(value):
        return lax.all_to_all(
            value, AXES, split_axis=0, concat_axis=0, tiled=True, axis_index_groups=groups
        )

    result = None
    seen = []
    for b in range(blocks):
        value = make_forward(places, density, y_forward, x_forward, b, owners, waves, stride, scale)
        seen.append(exchange(value))
    for b in range(blocks):
        value = mix_block(green, seen[b], order, b, devices, slab)
        if b == 0:
            together = lax.psum(seen[-1][:1, :1, :1, :LANES].astype(F32), AXES)
            value = after(value, together)
        value = lax.all_to_all(value, AXES, split_axis=0, concat_axis=0, tiled=True)
        result = make_inverse(value, x_inverse, y_inverse, b, result, scale)
    return result


def solution(mesh):
    in_specs = (
        P(AXES),
        P(None, AXES),
        P(None, AXES),
        P(AXES),
        P(AXES, None, None, None),
    )
    out_specs = P(AXES, None, None)

    def step(charges, cells, splines, counts, green):
        nx = green.shape[0]
        ny = green.shape[1] * LANES

        def body(*operands):
            return shards(nx, ny, *operands)

        return jax.shard_map(body, mesh=mesh, in_specs=in_specs, out_specs=out_specs, check_vma=False)(
            charges, cells, splines, counts, green
        )

    return step
```

time: 797 us -> 638 us (0.80)
  Pallas kernels: 0 us -> 278 us
  waiting for transfers between devices: 388 us -> 200 us
  matrix products: 137 us -> 0 us
  local copies, waits for them, and re-layouts: 129 us -> 12.4 us
  other arithmetic: 111 us -> 14.1 us
  blocking collectives: 0 us -> 91.3 us
  starting transfers between devices: 19.1 us -> 38.1 us
    pallas_call x0 -> x14, Pallas kernels: none -> 278 us  [the longest x4 115 us: make_forward(): pl.pallas_call(lambda places, *refs: forward_kernel(places, scale, *refs)...]
    all_to_all x4 -> x8, waiting for transfers between devices: 388 us -> 200 us  [the longest x4 135 us: shards(): value = lax.all_to_all(value, AXES, split_axis=0, concat_axis=0, tiled=True)]
    dot_general x9 -> x0, matrix products: 137 us -> none  [the longest x4 47.8 us: product(): return jnp.einsum(spec, left, right, preferred_element_type=jnp.float32)]
    scatter-add x1 -> x0, other arithmetic: 91.5 us -> none  [shards(): jnp.zeros((slab * NX * NY,), jnp.float32).at[cells.reshape(-1)]]
    psum x0 -> x1, blocking collectives: none -> 91.3 us  [shards(): together = lax.psum(seen[-1][:1, :1, :1, :LANES].astype(F32), AXES)]
    reshape x5 -> x2, local copies, waits for them, and re-layouts: 54.9 us -> 1.53 us  [the longest x1 0.77 us: shards(): both_values.reshape(2, -1, LANES)]
    convert_element_type x4 -> x0, local copies, waits for them, and re-layouts: 49.7 us -> none  [the longest x2 32.4 us: shards(): mixed = mixed.astype(jnp.bfloat16).reshape(devices, slab, 2, waves, width)]
    transpose x4 -> x0, local copies, waits for them, and re-layouts: 22.8 us -> none  [the longest x2 12.9 us: shards(): spectrum.reshape(slab, 2, devices, waves, width).transpose(2, 0, 1, 3, 4)]
  transfers between devices with their start and end apart: 4 -> 10, of which waited for: 4 -> 8; matrix products, arithmetic and copies ran while one was open for 22% -> 2% of each run, Pallas kernels for 0% -> 32%
where the time goes in v1:
time: 638 us; the launch traced here: 635 us
  Pallas kernels  278 us (44%)
  waiting for transfers between devices  200 us (31%)
  blocking collectives  91.3 us (14%)
  starting transfers between devices  38.1 us (6%)
  other arithmetic  14.1 us (2%)
  local copies, waits for them, and re-layouts  12.4 us (2%)
    all_to_all x4, waiting for transfers between devices, shards(): value = lax.all_to_all(value, AXES, split_axis=0, concat_axis=0, tiled=True)  135 us
    pallas_call x4, Pallas kernels, make_forward(): pl.pallas_call(lambda places, *refs: forward_kernel(places, scale, *refs)...  115 us
    psum x1, blocking collectives, shards(): together = lax.psum(seen[-1][:1, :1, :1, :LANES].astype(F32), AXES)  91.3 us
    pallas_call x4, Pallas kernels, mix_block(): pl.pallas_call(mix_kernel, out_shape=jax.ShapeDtypeStruct(shape, BF16), g...  66.4 us
    pallas_call x4, Pallas kernels, make_inverse(): pl.pallas_call(functools.partial(inverse_kernel, scale, first), out_shape...  66.4 us
    all_to_all x4, waiting for transfers between devices, exchange(): lax.all_to_all(value, AXES, split_axis=0, concat_axis=0, tiled=True, axis...  64.7 us
    pallas_call x1, Pallas kernels, make_density(): pl.pallas_call(density_kernel, out_shape=(shape, shape), grid_spec=pltpu....  29.6 us
    all_to_all x4, starting transfers between devices, exchange(): lax.all_to_all(value, AXES, split_axis=0, concat_axis=0, tiled=True, axis...  18 us
  transfers between devices with their start and end apart: 10, of which 8 were waited for; matrix products, arithmetic and copies ran while one was open for 2% of the time, Pallas kernels for 32%

profile of v1, /device:TPU:0, one launch (start us, length us, event | category | flops | bytes accessed | tf_op | source)
XLA Modules:
  0.0 634.6 jit_solution(7794492950824090293)
XLA Ops:
  3.1 6.4 %sort.15 = (s32[16384]{0:T(1024)S(1)}, f32[16384]{0:T(1024)S(1)}) sort(s32[16384]{0:T(1024)S(1)} %bitcast.20, f32[16384]{0:T(1024)S(1)} %bitcast.19), dimensions={0}, to_apply=%region_0.1 | sort | flops 229376 | bytes 262144 | tf_op jit(solution)/shard_map/sort | solution.py:305
  23.7 29.6 %density.1 = (bf16[24,512,512]{2,1,0:T(8,128)(2,1)}, bf16[24,512,512]{2,1,0:T(8,128)(2,1)}) custom-call(s32[2,49]{1,0:T(2,128)} %copy.13.starts, s32[2,132,128]{2,1,0:T(8,128)} %reshape.83.cells, f32[2,132,128]{2,1,0:T(8,128)} %reshape.84.values), custom_call_target="tpu_custom_call" | custom-call | flops 12884901888 | bytes 25165824 | tf_op jit(solution)/shard_map/density/pallas_call | solution.py:96
  53.8 28.8 %forward.7 = bf16[16,16,24,256]{3,2,1,0:T(8,128)(2,1)} custom-call(s32[24]{0:T(128)} %iota.26.places, bf16[24,512,512]{2,1,0:T(8,128)(2,1)} %get-tuple-element.11.refs_0_, bf16[24,512,512]{2,1,0:T(8,128)(2,1)} %get-tuple-element.12.refs_1_, bf16[1536,1024]{1,0:T(8,128)(2,1)} %constant.53.refs_2_, bf16[512,1536]{1,0:T(8,128)(2,1)} %maximum_maximum_fusion.refs_3_), custom_call_target="tpu_custom_call" | custom-call | flops 19327352832 | bytes 25165824 | tf_op jit(solution)/shard_map/forward/pallas_call | solution.py:150
  82.6 5.3 all-to-all-start.6
  88.3 28.8 %forward.6 = bf16[16,16,24,256]{3,2,1,0:T(8,128)(2,1)} custom-call(s32[24]{0:T(128)} %iota.25.places, bf16[24,512,512]{2,1,0:T(8,128)(2,1)} %get-tuple-element.11.refs_0_, bf16[24,512,512]{2,1,0:T(8,128)(2,1)} %get-tuple-element.12.refs_1_, bf16[1536,1024]{1,0:T(8,128)(2,1)} %constant.53.refs_2_, bf16[512,1536]{1,0:T(8,128)(2,1)} %maximum_maximum_fusion.refs_3_), custom_call_target="tpu_custom_call" | custom-call | flops 19327352832 | bytes 25165824 | tf_op jit(solution)/shard_map/forward/pallas_call | solution.py:150
  117.2 13.3 %all-to-all-done.6.seen_ref = bf16[16,16,24,256]{3,2,1,0:T(8,128)(2,1)S(1)} async-done(((bf16[16,16,24,256]{3,2,1,0:T(8,128)(2,1)}), bf16[16,16,24,256]{3,2,1,0:T(8,128)(2,1)S(1)}, u32[]{:S(2)}, u32[]{:S(2)}) %all-to-all-start.6) | async-done | bytes 3145760 | tf_op jit(solution)/shard_map/all_to_all | solution.py:358
  137.2 28.8 %forward.4 = bf16[16,16,24,256]{3,2,1,0:T(8,128)(2,1)} custom-call(s32[24]{0:T(128)} %iota.21.places, bf16[24,512,512]{2,1,0:T(8,128)(2,1)} %get-tuple-element.11.refs_0_, bf16[24,512,512]{2,1,0:T(8,128)(2,1)} %get-tuple-element.12.refs_1_, bf16[1536,1024]{1,0:T(8,128)(2,1)} %constant.53.refs_2_, bf16[512,1536]{1,0:T(8,128)(2,1)} %maximum_maximum_fusion.refs_3_), custom_call_target="tpu_custom_call" | custom-call | flops 19327352832 | bytes 25165824 | tf_op jit(solution)/shard_map/forward/pallas_call | solution.py:150
  166.0 13.2 %all-to-all-done.4.seen_ref = bf16[16,16,24,256]{3,2,1,0:T(8,128)(2,1)} async-done(((bf16[16,16,24,256]{3,2,1,0:T(8,128)(2,1)}), bf16[16,16,24,256]{3,2,1,0:T(8,128)(2,1)}, u32[]{:S(2)}, u32[]{:S(2)}) %all-to-all-start.4) | async-done | bytes 3145760 | tf_op jit(solution)/shard_map/all_to_all | solution.py:358
  183.6 28.8 %forward.5 = bf16[16,16,24,256]{3,2,1,0:T(8,128)(2,1)} custom-call(s32[24]{0:T(128)} %iota.24.places, bf16[24,512,512]{2,1,0:T(8,128)(2,1)} %get-tuple-element.11.refs_0_, bf16[24,512,512]{2,1,0:T(8,128)(2,1)} %get-tuple-element.12.refs_1_, bf16[1536,1024]{1,0:T(8,128)(2,1)} %constant.53.refs_2_, bf16[512,1536]{1,0:T(8,128)(2,1)} %maximum_maximum_fusion.refs_3_), custom_call_target="tpu_custom_call" | custom-call | flops 19327352832 | bytes 25165824 | tf_op jit(solution)/shard_map/forward/pallas_call | solution.py:150
  212.4 13.1 %all-to-all-done.seen_ref = bf16[16,16,24,256]{3,2,1,0:T(8,128)(2,1)S(1)} async-done(((bf16[16,16,24,256]{3,2,1,0:T(8,128)(2,1)}), bf16[16,16,24,256]{3,2,1,0:T(8,128)(2,1)S(1)}, u32[]{:S(2)}, u32[]{:S(2)}) %all-to-all-start) | async-done | bytes 3145760 | tf_op jit(solution)/shard_map/all_to_all | solution.py:358
  230.9 16.6 %mix.6 = bf16[32,12,16,256]{3,2,1,0:T(8,128)(2,1)} custom-call(bf16[16,4,384,384]{3,2,1,0:T(8,128)(2,1)} %green_ref.7, bf16[16,16,24,256]{3,2,1,0:T(8,128)(2,1)} %all-to-all-done.4.seen_ref, bf16[384,384]{1,0:T(8,128)(2,1)} %fusion.1.order_ref), custom_call_target="tpu_custom_call" | custom-call | flops 2415919104 | bytes 11010048 | tf_op jit(solution)/shard_map/mix/pallas_call | solution.py:210
  247.5 25.1 %all-to-all-done.2.seen_ref = bf16[16,16,24,256]{3,2,1,0:T(8,128)(2,1)} async-done(((bf16[16,16,24,256]{3,2,1,0:T(8,128)(2,1)}), bf16[16,16,24,256]{3,2,1,0:T(8,128)(2,1)}, u32[]{:S(2)}, u32[]{:S(2)}) %all-to-all-start.2) | async-done | bytes 3145760 | tf_op jit(solution)/shard_map/all_to_all | solution.py:358
  277.1 91.3 %psum.7.other_ref = f32[1,1,1,128]{3,2,1,0:T(1,128)} all-reduce(f32[1,1,1,128]{3,2,1,0:T(1,128)S(1)} %slice_convert_fusion), channel_id=1, replica_groups=mesh['zg'=2,'xy'=16] {'zg','xy'}, use_global_device_ids=true, to_apply=%region_2.3 | all-reduce | flops 128 | bytes 1024 | tf_op jit(solution)/shard_map/psum | solution.py:370
  368.4 16.6 %mix.7.value_ref = bf16[32,12,16,256]{3,2,1,0:T(8,128)(2,1)} custom-call(bf16[16,4,384,384]{3,2,1,0:T(8,128)(2,1)} %green_ref.7, bf16[16,16,24,256]{3,2,1,0:T(8,128)(2,1)} %copy-done.1, bf16[384,384]{1,0:T(8,128)(2,1)} %fusion.1.order_ref), custom_call_target="tpu_custom_call" | custom-call | flops 2415919104 | bytes 11010048 | tf_op jit(solution)/shard_map/mix/pallas_call | solution.py:210
  385.0 5.0 all-to-all-start.7
  390.0 16.6 %mix.5 = bf16[32,12,16,256]{3,2,1,0:T(8,128)(2,1)} custom-call(bf16[16,4,384,384]{3,2,1,0:T(8,128)(2,1)} %green_ref.7, bf16[16,16,24,256]{3,2,1,0:T(8,128)(2,1)} %all-to-all-done.2.seen_ref, bf16[384,384]{1,0:T(8,128)(2,1)} %fusion.1.order_ref), custom_call_target="tpu_custom_call" | custom-call | flops 2415919104 | bytes 11010048 | tf_op jit(solution)/shard_map/mix/pallas_call | solution.py:210
  406.6 55.8 %all-to-all-done.7.refs_0_ = bf16[32,12,16,256]{3,2,1,0:T(8,128)(2,1)S(1)} async-done(((bf16[32,12,16,256]{3,2,1,0:T(8,128)(2,1)}), bf16[32,12,16,256]{3,2,1,0:T(8,128)(2,1)S(1)}, u32[]{:S(2)}, u32[]{:S(2)}) %all-to-all-start.7) | async-done | bytes 3145760 | tf_op jit(solution)/shard_map/all_to_all | solution.py:372
  466.9 16.6 %mix.4 = bf16[32,12,16,256]{3,2,1,0:T(8,128)(2,1)} custom-call(bf16[16,4,384,384]{3,2,1,0:T(8,128)(2,1)} %green_ref.7, bf16[16,16,24,256]{3,2,1,0:T(8,128)(2,1)} %copy-done, bf16[384,384]{1,0:T(8,128)(2,1)} %fusion.1.order_ref), custom_call_target="tpu_custom_call" | custom-call | flops 2415919104 | bytes 11010048 | tf_op jit(solution)/shard_map/mix/pallas_call | solution.py:210
  483.5 55.9 %all-to-all-done.3.refs_0_ = bf16[32,12,16,256]{3,2,1,0:T(8,128)(2,1)S(1)} async-done(((bf16[32,12,16,256]{3,2,1,0:T(8,128)(2,1)}), bf16[32,12,16,256]{3,2,1,0:T(8,128)(2,1)S(1)}, u32[]{:S(2)}, u32[]{:S(2)}) %all-to-all-start.3) | async-done | bytes 3145760 | tf_op jit(solution)/shard_map/all_to_all | solution.py:372
  544.8 14.1 %inverse.4.refs_3_ = f32[12,512,512]{2,1,0:T(8,128)} custom-call(bf16[32,12,16,256]{3,2,1,0:T(8,128)(2,1)} %copy-done.3, bf16[1024,512]{1,0:T(8,128)(2,1)} %constant.66.refs_1_, bf16[4,256,512]{2,1,0:T(8,128)(2,1)} %constant.69.refs_2_), custom_call_target="tpu_custom_call" | custom-call | flops 4831838208 | bytes 25165824 | tf_op jit(solution)/shard_map/inverse/pallas_call | solution.py:264
  558.9 17.4 %inverse.5.refs_3_ = f32[12,512,512]{2,1,0:T(8,128)} custom-call(bf16[32,12,16,256]{3,2,1,0:T(8,128)(2,1)} %all-to-all-done.5.refs_0_, bf16[1024,512]{1,0:T(8,128)(2,1)} %constant.66.refs_1_, bf16[4,256,512]{2,1,0:T(8,128)(2,1)} %constant.69.refs_2_, f32[12,512,512]{2,1,0:T(8,128)} %inverse.4.refs_3_), custom_call_target="tpu_custom_call", output_to_operand_aliasing={{}: (3, {})} | custom-call | flops 4831838208 | bytes 25165824 | tf_op jit(solution)/shard_map/inverse/pallas_call | solution.py:264
  576.4 17.5 %inverse.6.refs_3_ = f32[12,512,512]{2,1,0:T(8,128)} custom-call(bf16[32,12,16,256]{3,2,1,0:T(8,128)(2,1)} %copy-done.2, bf16[1024,512]{1,0:T(8,128)(2,1)} %constant.66.refs_1_, bf16[4,256,512]{2,1,0:T(8,128)(2,1)} %constant.69.refs_2_, f32[12,512,512]{2,1,0:T(8,128)} %inverse.5.refs_3_), custom_call_target="tpu_custom_call", output_to_operand_aliasing={{}: (3, {})} | custom-call | flops 4831838208 | bytes 25165824 | tf_op jit(solution)/shard_map/inverse/pallas_call | solution.py:264
  593.8 23.3 %all-to-all-done.1.refs_0_ = bf16[32,12,16,256]{3,2,1,0:T(8,128)(2,1)} async-done(((bf16[32,12,16,256]{3,2,1,0:T(8,128)(2,1)}), bf16[32,12,16,256]{3,2,1,0:T(8,128)(2,1)}, u32[]{:S(2)}, u32[]{:S(2)}) %all-to-all-start.1) | async-done | bytes 3145760 | tf_op jit(solution)/shard_map/all_to_all | solution.py:372
  617.1 17.4 %inverse.7 = f32[12,512,512]{2,1,0:T(8,128)} custom-call(bf16[32,12,16,256]{3,2,1,0:T(8,128)(2,1)} %all-to-all-done.1.refs_0_, bf16[1024,512]{1,0:T(8,128)(2,1)} %constant.66.refs_1_, bf16[4,256,512]{2,1,0:T(8,128)(2,1)} %constant.69.refs_2_, f32[12,512,512]{2,1,0:T(8,128)} %inverse.6.refs_3_), custom_call_target="tpu_custom_call", output_to_operand_aliasing={{}: (3, {})} | custom-call | flops 4831838208 | bytes 25165824 | tf_op jit(solution)/shard_map/inverse/pallas_call | solution.py:264
  (44 shorter events, 48.1 us)
Async XLA Ops:
  9.5 7.8 %collective-permute-start = (s32[16384]{0:T(1024)S(1)}, s32[16384]{0:T(1024)S(1)}, u32[]{:S(2)}, u32[]{:S(2)}) collective-permute-start(s32[16384]{0:T(1024)S(1)} %get-tuple-element.9), channel_id=1, source_target_pairs={{0,8},{1,9},{2,10},{3,11},{4,12},{5,13},{6,14},{7,15},{8,0},{9,1},... | collective-permute-start | bytes 196616 | tf_op jit(solution)/shard_map/ppermute | solution.py:306
  13.7 9.0 %collective-permute-start.1 = (f32[16384]{0:T(1024)S(1)}, f32[16384]{0:T(1024)S(1)}, u32[]{:S(2)}, u32[]{:S(2)}) collective-permute-start(f32[16384]{0:T(1024)S(1)} %get-tuple-element.10), channel_id=1, source_target_pairs={{0,8},{1,9},{2,10},{3,11},{4,12},{5,13},{6,14},{7,15},{8,0},{9,1},... | collective-permute-start | bytes 196616 | tf_op jit(solution)/shard_map/ppermute | solution.py:307
  82.6 47.9 %all-to-all-start.6 = ((bf16[16,16,24,256]{3,2,1,0:T(8,128)(2,1)}), bf16[16,16,24,256]{3,2,1,0:T(8,128)(2,1)S(1)}, u32[]{:S(2)}, u32[]{:S(2)}) async-start(bf16[16,16,24,256]{3,2,1,0:T(8,128)(2,1)} %forward.7), calls=%async_computation.6 | async-start | bytes 6291456 | tf_op jit(solution)/shard_map/all_to_all | solution.py:358
  130.5 1.6 copy-start.1
  132.1 47.1 %all-to-all-start.4 = ((bf16[16,16,24,256]{3,2,1,0:T(8,128)(2,1)}), bf16[16,16,24,256]{3,2,1,0:T(8,128)(2,1)}, u32[]{:S(2)}, u32[]{:S(2)}) async-start(bf16[16,16,24,256]{3,2,1,0:T(8,128)(2,1)} %forward.6), calls=%async_computation.4 | async-start | bytes 6291456 | tf_op jit(solution)/shard_map/all_to_all | solution.py:358
  179.2 46.3 %all-to-all-start = ((bf16[16,16,24,256]{3,2,1,0:T(8,128)(2,1)}), bf16[16,16,24,256]{3,2,1,0:T(8,128)(2,1)S(1)}, u32[]{:S(2)}, u32[]{:S(2)}) async-start(bf16[16,16,24,256]{3,2,1,0:T(8,128)(2,1)} %forward.4), calls=%async_computation | async-start | bytes 6291456 | tf_op jit(solution)/shard_map/all_to_all | solution.py:358
  212.4 17.6 %copy-start.4 = (s32[384]{0:T(512)S(1)}, s32[384]{0:T(512)}, u32[]{:S(2)}) copy-start(s32[384]{0:T(512)} %constant.46.clone) | copy-start | bytes 4612
  225.5 51.5 %copy-start = (bf16[16,16,24,256]{3,2,1,0:T(8,128)(2,1)}, bf16[16,16,24,256]{3,2,1,0:T(8,128)(2,1)S(1)}, u32[]{:S(2)}) copy-start(bf16[16,16,24,256]{3,2,1,0:T(8,128)(2,1)S(1)} %all-to-all-done.seen_ref) | copy-start | bytes 9437188
  225.5 47.1 %all-to-all-start.2 = ((bf16[16,16,24,256]{3,2,1,0:T(8,128)(2,1)}), bf16[16,16,24,256]{3,2,1,0:T(8,128)(2,1)}, u32[]{:S(2)}, u32[]{:S(2)}) async-start(bf16[16,16,24,256]{3,2,1,0:T(8,128)(2,1)} %forward.5), calls=%async_computation.2 | async-start | bytes 6291456 | tf_op jit(solution)/shard_map/all_to_all | solution.py:358
  272.6 112.4 %all-to-all-start.5 = ((bf16[32,12,16,256]{3,2,1,0:T(8,128)(2,1)}), bf16[32,12,16,256]{3,2,1,0:T(8,128)(2,1)}, u32[]{:S(2)}, u32[]{:S(2)}) async-start(bf16[32,12,16,256]{3,2,1,0:T(8,128)(2,1)} %mix.6), calls=%async_computation.5 | async-start | bytes 6291456 | tf_op jit(solution)/shard_map/all_to_all | solution.py:372
  385.0 77.4 %all-to-all-start.7 = ((bf16[32,12,16,256]{3,2,1,0:T(8,128)(2,1)}), bf16[32,12,16,256]{3,2,1,0:T(8,128)(2,1)S(1)}, u32[]{:S(2)}, u32[]{:S(2)}) async-start(bf16[32,12,16,256]{3,2,1,0:T(8,128)(2,1)} %after.1), calls=%async_computation.7 | async-start | bytes 6291456 | tf_op jit(solution)/shard_map/all_to_all | solution.py:372
  462.4 1.7 copy-start.3
  464.1 75.3 %all-to-all-start.3 = ((bf16[32,12,16,256]{3,2,1,0:T(8,128)(2,1)}), bf16[32,12,16,256]{3,2,1,0:T(8,128)(2,1)S(1)}, u32[]{:S(2)}, u32[]{:S(2)}) async-start(bf16[32,12,16,256]{3,2,1,0:T(8,128)(2,1)} %mix.5), calls=%async_computation.3 | async-start | bytes 6291456 | tf_op jit(solution)/shard_map/all_to_all | solution.py:372
  539.4 1.6 copy-start.2
  541.1 76.1 %all-to-all-start.1 = ((bf16[32,12,16,256]{3,2,1,0:T(8,128)(2,1)}), bf16[32,12,16,256]{3,2,1,0:T(8,128)(2,1)}, u32[]{:S(2)}, u32[]{:S(2)}) async-start(bf16[32,12,16,256]{3,2,1,0:T(8,128)(2,1)} %mix.4), calls=%async_computation.1 | async-start | bytes 6291456 | tf_op jit(solution)/shard_map/all_to_all | solution.py:372

commit v2 on v1

--- a/solution.py
+++ b/solution.py
@@ -15,7 +15,7 @@
 LANES = 128
 POINTS = 512
 SIDE = 256
-VMEM = 60 * 2**20
+VMEM = 66_000_000
 AXES = ("zg", "xy")
 
 
@@ -227,17 +227,6 @@
     )(green, seen, order)
 
 
-def after(value, other):
-    return pl.pallas_call(
-        lambda value_ref, other_ref, out_ref: None,
-        out_shape=jax.ShapeDtypeStruct(value.shape, value.dtype),
-        in_specs=[pl.BlockSpec(memory_space=pl.ANY)] * 2,
-        out_specs=pl.BlockSpec(memory_space=pl.ANY),
-        input_output_aliases={0: 0},
-        name="after",
-    )(value, other)
-
-
 def inverse_kernel(scale, first, *refs):
     if first:
         seen_ref, x_table, y_table, out_ref = refs
@@ -366,9 +355,6 @@
         seen.append(exchange(value))
     for b in range(blocks):
         value = mix_block(green, seen[b], order, b, devices, slab)
-        if b == 0:
-            together = lax.psum(seen[-1][:1, :1, :1, :LANES].astype(F32), AXES)
-            value = after(value, together)
         value = lax.all_to_all(value, AXES, split_axis=0, concat_axis=0, tiled=True)
         result = make_inverse(value, x_inverse, y_inverse, b, result, scale)
     return result

time: 638 us -> 598 us (0.937)
  blocking collectives: 91.3 us -> 0 us
  waiting for transfers between devices: 200 us -> 256 us
    psum x1 -> x0, blocking collectives: 91.3 us -> none  [shards(): together = lax.psum(seen[-1][:1, :1, :1, :LANES].astype(F32), AXES)]
    all_to_all x4, waiting for transfers between devices: 135 us -> 191 us  [shards(): value = lax.all_to_all(value, AXES, split_axis=0, concat_axis=0, tiled=True)]
  transfers between devices with their start and end apart: 10 -> 10, of which waited for: 8 -> 9; matrix products, arithmetic and copies ran while one was open for 2% -> 2% of each run, Pallas kernels for 32% -> 34%
where the time goes in v2:
time: 598 us; the launch traced here: 595 us
  Pallas kernels  278 us (46%)
  waiting for transfers between devices  256 us (43%)
  starting transfers between devices  38.2 us (6%)
  other arithmetic  14.1 us (2%)
  local copies, waits for them, and re-layouts  7.44 us (1%)
    all_to_all x4, waiting for transfers between devices, shards(): value = lax.all_to_all(value, AXES, split_axis=0, concat_axis=0, tiled=True)  191 us
    pallas_call x4, Pallas kernels, make_forward(): pl.pallas_call(lambda places, *refs: forward_kernel(places, scale, *refs)...  115 us
    pallas_call x4, Pallas kernels, mix_block(): pl.pallas_call(mix_kernel, out_shape=jax.ShapeDtypeStruct(shape, BF16), g...  66.4 us
    pallas_call x4, Pallas kernels, make_inverse(): pl.pallas_call(functools.partial(inverse_kernel, scale, first), out_shape...  66.4 us
    all_to_all x4, waiting for transfers between devices, exchange(): lax.all_to_all(value, AXES, split_axis=0, concat_axis=0, tiled=True, axis...  65 us
    pallas_call x1, Pallas kernels, make_density(): pl.pallas_call(density_kernel, out_shape=(shape, shape), grid_spec=pltpu....  29.6 us
    all_to_all x4, starting transfers between devices, exchange(): lax.all_to_all(value, AXES, split_axis=0, concat_axis=0, tiled=True, axis...  18.8 us
    all_to_all x4, starting transfers between devices, shards(): value = lax.all_to_all(value, AXES, split_axis=0, concat_axis=0, tiled=True)  15.3 us
  transfers between devices with their start and end apart: 10, of which 9 were waited for; matrix products, arithmetic and copies ran while one was open for 2% of the time, Pallas kernels for 34%

profile of v2, /device:TPU:0, one launch (start us, length us, event | category | flops | bytes accessed | tf_op | source)
XLA Modules:
  0.0 594.5 jit_solution(16205338705265667887)
XLA Ops:
  3.1 6.4 %sort.15 = (s32[16384]{0:T(1024)S(1)}, f32[16384]{0:T(1024)S(1)}) sort(s32[16384]{0:T(1024)S(1)} %bitcast.20, f32[16384]{0:T(1024)S(1)} %bitcast.19), dimensions={0}, to_apply=%region_0.1 | sort | flops 229376 | bytes 262144 | tf_op jit(solution)/shard_map/sort | solution.py:294
  23.7 29.6 %density.1 = (bf16[24,512,512]{2,1,0:T(8,128)(2,1)}, bf16[24,512,512]{2,1,0:T(8,128)(2,1)}) custom-call(s32[2,49]{1,0:T(2,128)} %copy.12.starts, s32[2,132,128]{2,1,0:T(8,128)} %reshape.83.cells, f32[2,132,128]{2,1,0:T(8,128)} %reshape.84.values), custom_call_target="tpu_custom_call" | custom-call | flops 12884901888 | bytes 25165824 | tf_op jit(solution)/shard_map/density/pallas_call | solution.py:96
  53.8 28.9 %forward.7 = bf16[16,16,24,256]{3,2,1,0:T(8,128)(2,1)} custom-call(s32[24]{0:T(128)} %iota.26.places, bf16[24,512,512]{2,1,0:T(8,128)(2,1)} %get-tuple-element.11.refs_0_, bf16[24,512,512]{2,1,0:T(8,128)(2,1)} %get-tuple-element.12.refs_1_, bf16[1536,1024]{1,0:T(8,128)(2,1)} %constant.53.refs_2_, bf16[512,1536]{1,0:T(8,128)(2,1)} %maximum_maximum_fusion.refs_3_), custom_call_target="tpu_custom_call" | custom-call | flops 19327352832 | bytes 25165824 | tf_op jit(solution)/shard_map/forward/pallas_call | solution.py:150
  82.7 5.3 all-to-all-start.6
  88.6 28.8 %forward.6 = bf16[16,16,24,256]{3,2,1,0:T(8,128)(2,1)} custom-call(s32[24]{0:T(128)} %iota.25.places, bf16[24,512,512]{2,1,0:T(8,128)(2,1)} %get-tuple-element.11.refs_0_, bf16[24,512,512]{2,1,0:T(8,128)(2,1)} %get-tuple-element.12.refs_1_, bf16[1536,1024]{1,0:T(8,128)(2,1)} %constant.53.refs_2_, bf16[512,1536]{1,0:T(8,128)(2,1)} %maximum_maximum_fusion.refs_3_), custom_call_target="tpu_custom_call" | custom-call | flops 19327352832 | bytes 25165824 | tf_op jit(solution)/shard_map/forward/pallas_call | solution.py:150
  117.4 13.3 %all-to-all-done.6.seen_ref = bf16[16,16,24,256]{3,2,1,0:T(8,128)(2,1)} async-done(((bf16[16,16,24,256]{3,2,1,0:T(8,128)(2,1)}), bf16[16,16,24,256]{3,2,1,0:T(8,128)(2,1)}, u32[]{:S(2)}, u32[]{:S(2)}) %all-to-all-start.6) | async-done | bytes 3145760 | tf_op jit(solution)/shard_map/all_to_all | solution.py:347
  135.7 28.8 %forward.4 = bf16[16,16,24,256]{3,2,1,0:T(8,128)(2,1)} custom-call(s32[24]{0:T(128)} %iota.21.places, bf16[24,512,512]{2,1,0:T(8,128)(2,1)} %get-tuple-element.11.refs_0_, bf16[24,512,512]{2,1,0:T(8,128)(2,1)} %get-tuple-element.12.refs_1_, bf16[1536,1024]{1,0:T(8,128)(2,1)} %constant.53.refs_2_, bf16[512,1536]{1,0:T(8,128)(2,1)} %maximum_maximum_fusion.refs_3_), custom_call_target="tpu_custom_call" | custom-call | flops 19327352832 | bytes 25165824 | tf_op jit(solution)/shard_map/forward/pallas_call | solution.py:150
  164.5 13.3 %all-to-all-done.4.seen_ref = bf16[16,16,24,256]{3,2,1,0:T(8,128)(2,1)} async-done(((bf16[16,16,24,256]{3,2,1,0:T(8,128)(2,1)}), bf16[16,16,24,256]{3,2,1,0:T(8,128)(2,1)}, u32[]{:S(2)}, u32[]{:S(2)}) %all-to-all-start.4) | async-done | bytes 3145760 | tf_op jit(solution)/shard_map/all_to_all | solution.py:347
  182.8 28.9 %forward.5 = bf16[16,16,24,256]{3,2,1,0:T(8,128)(2,1)} custom-call(s32[24]{0:T(128)} %iota.24.places, bf16[24,512,512]{2,1,0:T(8,128)(2,1)} %get-tuple-element.11.refs_0_, bf16[24,512,512]{2,1,0:T(8,128)(2,1)} %get-tuple-element.12.refs_1_, bf16[1536,1024]{1,0:T(8,128)(2,1)} %constant.53.refs_2_, bf16[512,1536]{1,0:T(8,128)(2,1)} %maximum_maximum_fusion.refs_3_), custom_call_target="tpu_custom_call" | custom-call | flops 19327352832 | bytes 25165824 | tf_op jit(solution)/shard_map/forward/pallas_call | solution.py:150
  211.7 13.2 %all-to-all-done.seen_ref = bf16[16,16,24,256]{3,2,1,0:T(8,128)(2,1)} async-done(((bf16[16,16,24,256]{3,2,1,0:T(8,128)(2,1)}), bf16[16,16,24,256]{3,2,1,0:T(8,128)(2,1)}, u32[]{:S(2)}, u32[]{:S(2)}) %all-to-all-start) | async-done | bytes 3145760 | tf_op jit(solution)/shard_map/all_to_all | solution.py:347
  224.9 4.5 all-to-all-start.2
  230.2 16.6 %mix.7 = bf16[32,12,16,256]{3,2,1,0:T(8,128)(2,1)} custom-call(bf16[16,4,384,384]{3,2,1,0:T(8,128)(2,1)} %green_ref.7, bf16[16,16,24,256]{3,2,1,0:T(8,128)(2,1)} %all-to-all-done.6.seen_ref, bf16[384,384]{1,0:T(8,128)(2,1)} %fusion.1.order_ref), custom_call_target="tpu_custom_call" | custom-call | flops 2415919104 | bytes 11010048 | tf_op jit(solution)/shard_map/mix/pallas_call | solution.py:210
  246.8 25.2 %all-to-all-done.2.seen_ref = bf16[16,16,24,256]{3,2,1,0:T(8,128)(2,1)} async-done(((bf16[16,16,24,256]{3,2,1,0:T(8,128)(2,1)}), bf16[16,16,24,256]{3,2,1,0:T(8,128)(2,1)}, u32[]{:S(2)}, u32[]{:S(2)}) %all-to-all-start.2) | async-done | bytes 3145760 | tf_op jit(solution)/shard_map/all_to_all | solution.py:347
  276.4 16.6 %mix.6 = bf16[32,12,16,256]{3,2,1,0:T(8,128)(2,1)} custom-call(bf16[16,4,384,384]{3,2,1,0:T(8,128)(2,1)} %green_ref.7, bf16[16,16,24,256]{3,2,1,0:T(8,128)(2,1)} %all-to-all-done.4.seen_ref, bf16[384,384]{1,0:T(8,128)(2,1)} %fusion.1.order_ref), custom_call_target="tpu_custom_call" | custom-call | flops 2415919104 | bytes 11010048 | tf_op jit(solution)/shard_map/mix/pallas_call | solution.py:210
  293.0 55.8 %all-to-all-done.7.refs_0_ = bf16[32,12,16,256]{3,2,1,0:T(8,128)(2,1)} async-done(((bf16[32,12,16,256]{3,2,1,0:T(8,128)(2,1)}), bf16[32,12,16,256]{3,2,1,0:T(8,128)(2,1)}, u32[]{:S(2)}, u32[]{:S(2)}) %all-to-all-start.7) | async-done | bytes 3145760 | tf_op jit(solution)/shard_map/all_to_all | solution.py:358
  352.4 16.6 %mix.5 = bf16[32,12,16,256]{3,2,1,0:T(8,128)(2,1)} custom-call(bf16[16,4,384,384]{3,2,1,0:T(8,128)(2,1)} %green_ref.7, bf16[16,16,24,256]{3,2,1,0:T(8,128)(2,1)} %all-to-all-done.2.seen_ref, bf16[384,384]{1,0:T(8,128)(2,1)} %fusion.1.order_ref), custom_call_target="tpu_custom_call" | custom-call | flops 2415919104 | bytes 11010048 | tf_op jit(solution)/shard_map/mix/pallas_call | solution.py:210
  369.0 55.9 %all-to-all-done.5.refs_0_ = bf16[32,12,16,256]{3,2,1,0:T(8,128)(2,1)} async-done(((bf16[32,12,16,256]{3,2,1,0:T(8,128)(2,1)}), bf16[32,12,16,256]{3,2,1,0:T(8,128)(2,1)}, u32[]{:S(2)}, u32[]{:S(2)}) %all-to-all-start.5) | async-done | bytes 3145760 | tf_op jit(solution)/shard_map/all_to_all | solution.py:358
  428.5 16.6 %mix.4 = bf16[32,12,16,256]{3,2,1,0:T(8,128)(2,1)} custom-call(bf16[16,4,384,384]{3,2,1,0:T(8,128)(2,1)} %green_ref.7, bf16[16,16,24,256]{3,2,1,0:T(8,128)(2,1)} %all-to-all-done.seen_ref, bf16[384,384]{1,0:T(8,128)(2,1)} %fusion.1.order_ref), custom_call_target="tpu_custom_call" | custom-call | flops 2415919104 | bytes 11010048 | tf_op jit(solution)/shard_map/mix/pallas_call | solution.py:210
  445.1 55.9 %all-to-all-done.3.refs_0_ = bf16[32,12,16,256]{3,2,1,0:T(8,128)(2,1)} async-done(((bf16[32,12,16,256]{3,2,1,0:T(8,128)(2,1)}), bf16[32,12,16,256]{3,2,1,0:T(8,128)(2,1)}, u32[]{:S(2)}, u32[]{:S(2)}) %all-to-all-start.3) | async-done | bytes 3145760 | tf_op jit(solution)/shard_map/all_to_all | solution.py:358
  504.8 14.1 %inverse.4.refs_3_ = f32[12,512,512]{2,1,0:T(8,128)} custom-call(bf16[32,12,16,256]{3,2,1,0:T(8,128)(2,1)} %all-to-all-done.7.refs_0_, bf16[1024,512]{1,0:T(8,128)(2,1)} %constant.66.refs_1_, bf16[4,256,512]{2,1,0:T(8,128)(2,1)} %constant.69.refs_2_), custom_call_target="tpu_custom_call" | custom-call | flops 4831838208 | bytes 25165824 | tf_op jit(solution)/shard_map/inverse/pallas_call | solution.py:253
  518.9 17.4 %inverse.5.refs_3_ = f32[12,512,512]{2,1,0:T(8,128)} custom-call(bf16[32,12,16,256]{3,2,1,0:T(8,128)(2,1)} %all-to-all-done.5.refs_0_, bf16[1024,512]{1,0:T(8,128)(2,1)} %constant.66.refs_1_, bf16[4,256,512]{2,1,0:T(8,128)(2,1)} %constant.69.refs_2_, f32[12,512,512]{2,1,0:T(8,128)} %inverse.4.refs_3_), custom_call_target="tpu_custom_call", output_to_operand_aliasing={{}: (3, {})} | custom-call | flops 4831838208 | bytes 25165824 | tf_op jit(solution)/shard_map/inverse/pallas_call | solution.py:253
  536.3 17.5 %inverse.6.refs_3_ = f32[12,512,512]{2,1,0:T(8,128)} custom-call(bf16[32,12,16,256]{3,2,1,0:T(8,128)(2,1)} %all-to-all-done.3.refs_0_, bf16[1024,512]{1,0:T(8,128)(2,1)} %constant.66.refs_1_, bf16[4,256,512]{2,1,0:T(8,128)(2,1)} %constant.69.refs_2_, f32[12,512,512]{2,1,0:T(8,128)} %inverse.5.refs_3_), custom_call_target="tpu_custom_call", output_to_operand_aliasing={{}: (3, {})} | custom-call | flops 4831838208 | bytes 25165824 | tf_op jit(solution)/shard_map/inverse/pallas_call | solution.py:253
  553.8 23.3 %all-to-all-done.1.refs_0_ = bf16[32,12,16,256]{3,2,1,0:T(8,128)(2,1)} async-done(((bf16[32,12,16,256]{3,2,1,0:T(8,128)(2,1)}), bf16[32,12,16,256]{3,2,1,0:T(8,128)(2,1)}, u32[]{:S(2)}, u32[]{:S(2)}) %all-to-all-start.1) | async-done | bytes 3145760 | tf_op jit(solution)/shard_map/all_to_all | solution.py:358
  577.1 17.4 %inverse.7 = f32[12,512,512]{2,1,0:T(8,128)} custom-call(bf16[32,12,16,256]{3,2,1,0:T(8,128)(2,1)} %all-to-all-done.1.refs_0_, bf16[1024,512]{1,0:T(8,128)(2,1)} %constant.66.refs_1_, bf16[4,256,512]{2,1,0:T(8,128)(2,1)} %constant.69.refs_2_, f32[12,512,512]{2,1,0:T(8,128)} %inverse.6.refs_3_), custom_call_target="tpu_custom_call", output_to_operand_aliasing={{}: (3, {})} | custom-call | flops 4831838208 | bytes 25165824 | tf_op jit(solution)/shard_map/inverse/pallas_call | solution.py:253
  (33 shorter events, 43.7 us)
Async XLA Ops:
  9.5 7.8 %collective-permute-start = (s32[16384]{0:T(1024)S(1)}, s32[16384]{0:T(1024)S(1)}, u32[]{:S(2)}, u32[]{:S(2)}) collective-permute-start(s32[16384]{0:T(1024)S(1)} %get-tuple-element.9), channel_id=1, source_target_pairs={{0,8},{1,9},{2,10},{3,11},{4,12},{5,13},{6,14},{7,15},{8,0},{9,1},... | collective-permute-start | bytes 196616 | tf_op jit(solution)/shard_map/ppermute | solution.py:295
  13.7 9.0 %collective-permute-start.1 = (f32[16384]{0:T(1024)S(1)}, f32[16384]{0:T(1024)S(1)}, u32[]{:S(2)}, u32[]{:S(2)}) collective-permute-start(f32[16384]{0:T(1024)S(1)} %get-tuple-element.10), channel_id=1, source_target_pairs={{0,8},{1,9},{2,10},{3,11},{4,12},{5,13},{6,14},{7,15},{8,0},{9,1},... | collective-permute-start | bytes 196616 | tf_op jit(solution)/shard_map/ppermute | solution.py:296
  82.7 48.0 %all-to-all-start.6 = ((bf16[16,16,24,256]{3,2,1,0:T(8,128)(2,1)}), bf16[16,16,24,256]{3,2,1,0:T(8,128)(2,1)}, u32[]{:S(2)}, u32[]{:S(2)}) async-start(bf16[16,16,24,256]{3,2,1,0:T(8,128)(2,1)} %forward.7), calls=%async_computation.6 | async-start | bytes 6291456 | tf_op jit(solution)/shard_map/all_to_all | solution.py:347
  130.7 47.1 %all-to-all-start.4 = ((bf16[16,16,24,256]{3,2,1,0:T(8,128)(2,1)}), bf16[16,16,24,256]{3,2,1,0:T(8,128)(2,1)}, u32[]{:S(2)}, u32[]{:S(2)}) async-start(bf16[16,16,24,256]{3,2,1,0:T(8,128)(2,1)} %forward.6), calls=%async_computation.4 | async-start | bytes 6291456 | tf_op jit(solution)/shard_map/all_to_all | solution.py:347
  177.8 47.1 %all-to-all-start = ((bf16[16,16,24,256]{3,2,1,0:T(8,128)(2,1)}), bf16[16,16,24,256]{3,2,1,0:T(8,128)(2,1)}, u32[]{:S(2)}, u32[]{:S(2)}) async-start(bf16[16,16,24,256]{3,2,1,0:T(8,128)(2,1)} %forward.4), calls=%async_computation | async-start | bytes 6291456 | tf_op jit(solution)/shard_map/all_to_all | solution.py:347
  211.7 17.7 %copy-start = (s32[384]{0:T(512)S(1)}, s32[384]{0:T(512)}, u32[]{:S(2)}) copy-start(s32[384]{0:T(512)} %constant.46.clone) | copy-start | bytes 4612
  224.9 47.1 %all-to-all-start.2 = ((bf16[16,16,24,256]{3,2,1,0:T(8,128)(2,1)}), bf16[16,16,24,256]{3,2,1,0:T(8,128)(2,1)}, u32[]{:S(2)}, u32[]{:S(2)}) async-start(bf16[16,16,24,256]{3,2,1,0:T(8,128)(2,1)} %forward.5), calls=%async_computation.2 | async-start | bytes 6291456 | tf_op jit(solution)/shard_map/all_to_all | solution.py:347
  272.0 76.9 %all-to-all-start.7 = ((bf16[32,12,16,256]{3,2,1,0:T(8,128)(2,1)}), bf16[32,12,16,256]{3,2,1,0:T(8,128)(2,1)}, u32[]{:S(2)}, u32[]{:S(2)}) async-start(bf16[32,12,16,256]{3,2,1,0:T(8,128)(2,1)} %mix.7), calls=%async_computation.7 | async-start | bytes 6291456 | tf_op jit(solution)/shard_map/all_to_all | solution.py:358
  348.9 76.1 %all-to-all-start.5 = ((bf16[32,12,16,256]{3,2,1,0:T(8,128)(2,1)}), bf16[32,12,16,256]{3,2,1,0:T(8,128)(2,1)}, u32[]{:S(2)}, u32[]{:S(2)}) async-start(bf16[32,12,16,256]{3,2,1,0:T(8,128)(2,1)} %mix.6), calls=%async_computation.5 | async-start | bytes 6291456 | tf_op jit(solution)/shard_map/all_to_all | solution.py:358
  424.9 76.1 %all-to-all-start.3 = ((bf16[32,12,16,256]{3,2,1,0:T(8,128)(2,1)}), bf16[32,12,16,256]{3,2,1,0:T(8,128)(2,1)}, u32[]{:S(2)}, u32[]{:S(2)}) async-start(bf16[32,12,16,256]{3,2,1,0:T(8,128)(2,1)} %mix.5), calls=%async_computation.3 | async-start | bytes 6291456 | tf_op jit(solution)/shard_map/all_to_all | solution.py:358
  501.0 76.1 %all-to-all-start.1 = ((bf16[32,12,16,256]{3,2,1,0:T(8,128)(2,1)}), bf16[32,12,16,256]{3,2,1,0:T(8,128)(2,1)}, u32[]{:S(2)}, u32[]{:S(2)}) async-start(bf16[32,12,16,256]{3,2,1,0:T(8,128)(2,1)} %mix.4), calls=%async_computation.1 | async-start | bytes 6291456 | tf_op jit(solution)/shard_map/all_to_all | solution.py:358
